TPU v7x, 128 devices: a whole 4x4x4 slice. The times are simulated.
128 devices in a mesh: batch: 1, cols: 2 (over core), rows: 64 (over z, y, x).
Axes of the slice: x: 4, y: 4, z: 4, core: 2. Of those that a mesh axis runs over, the one named last changes fastest.
Arguments:
- frames: bfloat16 [16, 2, 2048, 64, 64], P(None, 'batch', 'rows', 'cols')
- w_x: bfloat16 [3, 3, 64, 256], replicated
- w_h: bfloat16 [3, 3, 64, 256], replicated
- gate_bias: float32 [256], replicated
- h_init: bfloat16 [2, 2048, 64, 64], P('batch', 'rows', 'cols')
- c_init: float32 [2, 2048, 64, 64], P('batch', 'rows', 'cols')
Outputs:
- output 1: bfloat16 [16, 2, 2048, 64, 64], P(None, 'batch', 'rows', 'cols')
- output 2: float32 [2, 2048, 64, 64], P('batch', 'rows', 'cols')
All inputs are finite; a program needn't handle non-finite values.
Results may differ from a plain program's by a relative error of at most 0.00242049.
Values are sent between devices in bfloat16 or wider.
A program may use at most 1 GiB of HBM per device.

v0:
```python
import jax
import jax.numpy as jnp
from jax import lax
from jax.sharding import PartitionSpec as P, NamedSharding


def edge_swap(tile_arr, halo_width, split_dim, axis_label, axis_count):
    length = tile_arr.shape[split_dim]
    low_edge = lax.slice_in_dim(tile_arr, 0, halo_width, axis=split_dim)
    high_edge = lax.slice_in_dim(tile_arr, length - halo_width, length, axis=split_dim)
    down_pairs = [(source, source + 1) for source in range(axis_count - 1)]
    up_pairs = [(source + 1, source) for source in range(axis_count - 1)]
    from_prev = lax.ppermute(high_edge, axis_label, down_pairs)
    from_next = lax.ppermute(low_edge, axis_label, up_pairs)
    return jnp.concatenate([from_prev, tile_arr, from_next], axis=split_dim)


def with_halo(tile_arr, halo_width, row_dim, row_count, col_count):
    row_ext = edge_swap(tile_arr, halo_width, row_dim, "rows", row_count)
    return edge_swap(row_ext, halo_width, row_dim + 1, "cols", col_count)


def conv_taps(padded, weights, out_rows, out_cols):
    tap_list = [padded[:, row_off:row_off + out_rows, col_off:col_off + out_cols, :] for row_off in range(3) for col_off in range(3)]
    patches = jnp.concatenate(tap_list, axis=-1)
    flat_patches = patches.reshape(-1, patches.shape[-1])
    flat_weights = weights.reshape(-1, weights.shape[-1])
    product = jnp.dot(flat_patches, flat_weights, preferred_element_type=jnp.float32)
    return product.reshape(padded.shape[0], out_rows, out_cols, -1)


def lstm_cell(gate_sum, cell_prev):
    hidden_width = cell_prev.shape[-1]
    in_gate = jax.nn.sigmoid(gate_sum[..., :hidden_width])
    forget_gate = jax.nn.sigmoid(gate_sum[..., hidden_width:2 * hidden_width])
    out_gate = jax.nn.sigmoid(gate_sum[..., 2 * hidden_width:3 * hidden_width])
    cand_gate = jnp.tanh(gate_sum[..., 3 * hidden_width:])
    cell_next = forget_gate * cell_prev + in_gate * cand_gate
    hidden_next = (out_gate * jnp.tanh(cell_next)).astype(jnp.bfloat16)
    return hidden_next, cell_next


def solution(mesh):
    row_count = mesh.shape["rows"]
    col_count = mesh.shape["cols"]
    frame_spec = P(None, "batch", "rows", "cols", None)
    state_spec = P("batch", "rows", "cols", None)

    def local_run(frames, w_x, w_h, gate_bias, h_init, c_init):
        tile_rows = h_init.shape[1]
        tile_cols = h_init.shape[2]
        frames_ext = with_halo(frames, 1, 2, row_count, col_count)

        def step_fn(state_pair, frame_ext):
            hidden, cell_state = state_pair
            hidden_ext = with_halo(hidden, 1, 1, row_count, col_count)
            gate_sum = conv_taps(frame_ext, w_x, tile_rows, tile_cols) + conv_taps(hidden_ext, w_h, tile_rows, tile_cols) + gate_bias
            hidden_next, cell_next = lstm_cell(gate_sum, cell_state)
            return (hidden_next, cell_next), hidden_next

        final_pair, all_hidden = lax.scan(step_fn, (h_init, c_init), frames_ext)
        return all_hidden, final_pair[1]

    return jax.shard_map(local_run, mesh=mesh, in_specs=(frame_spec, P(), P(), P(), state_spec, state_spec), out_specs=(frame_spec, state_spec), check_vma=False)
```

profile of v0, /device:TPU:97, one launch (start us, length us, event | category | flops | bytes accessed | tf_op | source)
XLA Modules:
  0.0 776.3 jit_solution(13590870260494841416)
XLA Ops:
  7.5 6.4 collective-permute-start.5
  18.2 16.4 %constant_dynamic-update-slice_fusion.4 = bf16[16,2,34,32,64]{4,0,3,2,1:T(8,128)(2,1)} fusion(bf16[16,2,34,32,64]{4,0,3,2,1:T(8,128)(2,1)} %constant_dynamic-update-slice_fusion.5, bf16[16,2,32,32,64]{4,3,2,1,0:T(8,128)(2,1)} %param.8), kind=kLoop, calls=%fused_computation.42 | loop fusion | bytes 16777216
  43.0 6.1 pad_maximum_fusion.4
  49.1 5.8 copy.11
  55.0 721.4 %while.14 = (s32[]{:T(128)}, bf16[2,32,32,64]{3,2,1,0:T(8,128)(2,1)S(1)}, f32[2,32,32,64]{3,2,1,0:T(8,128)}, bf16[16,2,32,32,64]{4,3,2,1,0:T(8,128)(2,1)}, bf16[...) while((s32[]{:T(128)}, ...), condition=%wide.region_1.2_spmd, body=%wide.region_0.1_spmd.sunk | while | flops 1215037440 | bytes 36178216 | solution.py:61
  56.9 7.6 collective-permute-start
  68.0 5.3 concatenate.36
  100.7 7.6 collective-permute-start
  111.9 5.3 concatenate.36
  145.9 7.6 collective-permute-start
  157.0 5.3 concatenate.36
  191.1 7.6 collective-permute-start
  236.2 7.6 collective-permute-start
  281.4 7.6 collective-permute-start
  326.6 7.6 collective-permute-start
  371.7 7.6 collective-permute-start
  416.9 7.6 collective-permute-start
  462.1 7.6 collective-permute-start
  507.2 7.6 collective-permute-start
  552.4 7.6 collective-permute-start
  597.6 7.6 collective-permute-start
  642.7 7.6 collective-permute-start
  687.9 7.6 collective-permute-start
  733.1 7.6 collective-permute-start
  (370 shorter events, 602.2 us)
Async XLA Ops:
  7.5 27.1 %collective-permute-start.5 = (bf16[16,2,1,32,64]{4,0,3,2,1:T(8,128)(2,1)S(1)}, bf16[16,2,1,32,64]{4,0,3,2,1:T(8,128)(2,1)S(1)}, u32[]{:S(2)}, u32[]{:S(2)}) collective-permute-start(bf16[16,2,1,32,64]{4,0,3,2,1:T(8,128)(2,1)S(1)} %copy.16), channel_id=1, source_target_pairs={{1,0},{2,1},{3,2},{4,3},{5,4},{6,5},{7,6},{8,7},{9,8},{10,9},{11,1... | collective-permute-start | bytes 393224 | tf_op jit(solution)/shard_map/ppermute | solution.py:14
  55.0 18.4 %collective-permute-start.1 = (bf16[2,1,32,64]{3,2,1,0:T(8,128)(2,1)S(1)}, bf16[2,1,32,64]{3,2,1,0:T(8,128)(2,1)S(1)}, u32[]{:S(2)}, u32[]{:S(2)}) collective-permute-start(bf16[2,1,32,64]{3,2,1,0:T(8,128)(2,1)S(1)} %get-tuple-element.187), channel_id=1, source_target_pairs={{0,1},{1,2},{2,3},{3,4},{4,5},{5,6},{6,7},{7,8},{8,9},{9,10},{10,1... | collective-permute-start | bytes 24584 | tf_op jit(solution)/shard_map/while/body/eval_jaxpr/ppermute | solution.py:13
  56.9 16.5 %collective-permute-start = (bf16[2,1,32,64]{3,2,1,0:T(8,128)(2,1)S(1)}, bf16[2,1,32,64]{3,2,1,0:T(8,128)(2,1)S(1)}, u32[]{:S(2)}, u32[]{:S(2)}) collective-permute-start(bf16[2,1,32,64]{3,2,1,0:T(8,128)(2,1)S(1)} %get-tuple-element.186), channel_id=1, source_target_pairs={{1,0},{2,1},{3,2},{4,3},{5,4},{6,5},{7,6},{8,7},{9,8},{10,9},{11,1... | collective-permute-start | bytes 24584 | tf_op jit(solution)/shard_map/while/body/eval_jaxpr/ppermute | solution.py:14
  98.8 18.4 %collective-permute-start.1 = (bf16[2,1,32,64]{3,2,1,0:T(8,128)(2,1)S(1)}, bf16[2,1,32,64]{3,2,1,0:T(8,128)(2,1)S(1)}, u32[]{:S(2)}, u32[]{:S(2)}) collective-permute-start(bf16[2,1,32,64]{3,2,1,0:T(8,128)(2,1)S(1)} %get-tuple-element.187), channel_id=1, source_target_pairs={{0,1},{1,2},{2,3},{3,4},{4,5},{5,6},{6,7},{7,8},{8,9},{9,10},{10,1... | collective-permute-start | bytes 24584 | tf_op jit(solution)/shard_map/while/body/eval_jaxpr/ppermute | solution.py:13
  100.7 16.5 %collective-permute-start = (bf16[2,1,32,64]{3,2,1,0:T(8,128)(2,1)S(1)}, bf16[2,1,32,64]{3,2,1,0:T(8,128)(2,1)S(1)}, u32[]{:S(2)}, u32[]{:S(2)}) collective-permute-start(bf16[2,1,32,64]{3,2,1,0:T(8,128)(2,1)S(1)} %get-tuple-element.186), channel_id=1, source_target_pairs={{1,0},{2,1},{3,2},{4,3},{5,4},{6,5},{7,6},{8,7},{9,8},{10,9},{11,1... | collective-permute-start | bytes 24584 | tf_op jit(solution)/shard_map/while/body/eval_jaxpr/ppermute | solution.py:14
  144.0 18.4 %collective-permute-start.1 = (bf16[2,1,32,64]{3,2,1,0:T(8,128)(2,1)S(1)}, bf16[2,1,32,64]{3,2,1,0:T(8,128)(2,1)S(1)}, u32[]{:S(2)}, u32[]{:S(2)}) collective-permute-start(bf16[2,1,32,64]{3,2,1,0:T(8,128)(2,1)S(1)} %get-tuple-element.187), channel_id=1, source_target_pairs={{0,1},{1,2},{2,3},{3,4},{4,5},{5,6},{6,7},{7,8},{8,9},{9,10},{10,1... | collective-permute-start | bytes 24584 | tf_op jit(solution)/shard_map/while/body/eval_jaxpr/ppermute | solution.py:13
  145.9 16.5 %collective-permute-start = (bf16[2,1,32,64]{3,2,1,0:T(8,128)(2,1)S(1)}, bf16[2,1,32,64]{3,2,1,0:T(8,128)(2,1)S(1)}, u32[]{:S(2)}, u32[]{:S(2)}) collective-permute-start(bf16[2,1,32,64]{3,2,1,0:T(8,128)(2,1)S(1)} %get-tuple-element.186), channel_id=1, source_target_pairs={{1,0},{2,1},{3,2},{4,3},{5,4},{6,5},{7,6},{8,7},{9,8},{10,9},{11,1... | collective-permute-start | bytes 24584 | tf_op jit(solution)/shard_map/while/body/eval_jaxpr/ppermute | solution.py:14
  189.1 18.4 %collective-permute-start.1 = (bf16[2,1,32,64]{3,2,1,0:T(8,128)(2,1)S(1)}, bf16[2,1,32,64]{3,2,1,0:T(8,128)(2,1)S(1)}, u32[]{:S(2)}, u32[]{:S(2)}) collective-permute-start(bf16[2,1,32,64]{3,2,1,0:T(8,128)(2,1)S(1)} %get-tuple-element.187), channel_id=1, source_target_pairs={{0,1},{1,2},{2,3},{3,4},{4,5},{5,6},{6,7},{7,8},{8,9},{9,10},{10,1... | collective-permute-start | bytes 24584 | tf_op jit(solution)/shard_map/while/body/eval_jaxpr/ppermute | solution.py:13
  234.3 18.4 %collective-permute-start.1 = (bf16[2,1,32,64]{3,2,1,0:T(8,128)(2,1)S(1)}, bf16[2,1,32,64]{3,2,1,0:T(8,128)(2,1)S(1)}, u32[]{:S(2)}, u32[]{:S(2)}) collective-permute-start(bf16[2,1,32,64]{3,2,1,0:T(8,128)(2,1)S(1)} %get-tuple-element.187), channel_id=1, source_target_pairs={{0,1},{1,2},{2,3},{3,4},{4,5},{5,6},{6,7},{7,8},{8,9},{9,10},{10,1... | collective-permute-start | bytes 24584 | tf_op jit(solution)/shard_map/while/body/eval_jaxpr/ppermute | solution.py:13
  236.2 16.5 %collective-permute-start = (bf16[2,1,32,64]{3,2,1,0:T(8,128)(2,1)S(1)}, bf16[2,1,32,64]{3,2,1,0:T(8,128)(2,1)S(1)}, u32[]{:S(2)}, u32[]{:S(2)}) collective-permute-start(bf16[2,1,32,64]{3,2,1,0:T(8,128)(2,1)S(1)} %get-tuple-element.186), channel_id=1, source_target_pairs={{1,0},{2,1},{3,2},{4,3},{5,4},{6,5},{7,6},{8,7},{9,8},{10,9},{11,1... | collective-permute-start | bytes 24584 | tf_op jit(solution)/shard_map/while/body/eval_jaxpr/ppermute | solution.py:14
  279.5 18.4 %collective-permute-start.1 = (bf16[2,1,32,64]{3,2,1,0:T(8,128)(2,1)S(1)}, bf16[2,1,32,64]{3,2,1,0:T(8,128)(2,1)S(1)}, u32[]{:S(2)}, u32[]{:S(2)}) collective-permute-start(bf16[2,1,32,64]{3,2,1,0:T(8,128)(2,1)S(1)} %get-tuple-element.187), channel_id=1, source_target_pairs={{0,1},{1,2},{2,3},{3,4},{4,5},{5,6},{6,7},{7,8},{8,9},{9,10},{10,1... | collective-permute-start | bytes 24584 | tf_op jit(solution)/shard_map/while/body/eval_jaxpr/ppermute | solution.py:13
  324.7 18.4 %collective-permute-start.1 = (bf16[2,1,32,64]{3,2,1,0:T(8,128)(2,1)S(1)}, bf16[2,1,32,64]{3,2,1,0:T(8,128)(2,1)S(1)}, u32[]{:S(2)}, u32[]{:S(2)}) collective-permute-start(bf16[2,1,32,64]{3,2,1,0:T(8,128)(2,1)S(1)} %get-tuple-element.187), channel_id=1, source_target_pairs={{0,1},{1,2},{2,3},{3,4},{4,5},{5,6},{6,7},{7,8},{8,9},{9,10},{10,1... | collective-permute-start | bytes 24584 | tf_op jit(solution)/shard_map/while/body/eval_jaxpr/ppermute | solution.py:13
  326.6 16.5 %collective-permute-start = (bf16[2,1,32,64]{3,2,1,0:T(8,128)(2,1)S(1)}, bf16[2,1,32,64]{3,2,1,0:T(8,128)(2,1)S(1)}, u32[]{:S(2)}, u32[]{:S(2)}) collective-permute-start(bf16[2,1,32,64]{3,2,1,0:T(8,128)(2,1)S(1)} %get-tuple-element.186), channel_id=1, source_target_pairs={{1,0},{2,1},{3,2},{4,3},{5,4},{6,5},{7,6},{8,7},{9,8},{10,9},{11,1... | collective-permute-start | bytes 24584 | tf_op jit(solution)/shard_map/while/body/eval_jaxpr/ppermute | solution.py:14
  369.8 18.4 %collective-permute-start.1 = (bf16[2,1,32,64]{3,2,1,0:T(8,128)(2,1)S(1)}, bf16[2,1,32,64]{3,2,1,0:T(8,128)(2,1)S(1)}, u32[]{:S(2)}, u32[]{:S(2)}) collective-permute-start(bf16[2,1,32,64]{3,2,1,0:T(8,128)(2,1)S(1)} %get-tuple-element.187), channel_id=1, source_target_pairs={{0,1},{1,2},{2,3},{3,4},{4,5},{5,6},{6,7},{7,8},{8,9},{9,10},{10,1... | collective-permute-start | bytes 24584 | tf_op jit(solution)/shard_map/while/body/eval_jaxpr/ppermute | solution.py:13
  371.7 16.5 %collective-permute-start = (bf16[2,1,32,64]{3,2,1,0:T(8,128)(2,1)S(1)}, bf16[2,1,32,64]{3,2,1,0:T(8,128)(2,1)S(1)}, u32[]{:S(2)}, u32[]{:S(2)}) collective-permute-start(bf16[2,1,32,64]{3,2,1,0:T(8,128)(2,1)S(1)} %get-tuple-element.186), channel_id=1, source_target_pairs={{1,0},{2,1},{3,2},{4,3},{5,4},{6,5},{7,6},{8,7},{9,8},{10,9},{11,1... | collective-permute-start | bytes 24584 | tf_op jit(solution)/shard_map/while/body/eval_jaxpr/ppermute | solution.py:14
  415.0 18.4 %collective-permute-start.1 = (bf16[2,1,32,64]{3,2,1,0:T(8,128)(2,1)S(1)}, bf16[2,1,32,64]{3,2,1,0:T(8,128)(2,1)S(1)}, u32[]{:S(2)}, u32[]{:S(2)}) collective-permute-start(bf16[2,1,32,64]{3,2,1,0:T(8,128)(2,1)S(1)} %get-tuple-element.187), channel_id=1, source_target_pairs={{0,1},{1,2},{2,3},{3,4},{4,5},{5,6},{6,7},{7,8},{8,9},{9,10},{10,1... | collective-permute-start | bytes 24584 | tf_op jit(solution)/shard_map/while/body/eval_jaxpr/ppermute | solution.py:13
  416.9 16.5 %collective-permute-start = (bf16[2,1,32,64]{3,2,1,0:T(8,128)(2,1)S(1)}, bf16[2,1,32,64]{3,2,1,0:T(8,128)(2,1)S(1)}, u32[]{:S(2)}, u32[]{:S(2)}) collective-permute-start(bf16[2,1,32,64]{3,2,1,0:T(8,128)(2,1)S(1)} %get-tuple-element.186), channel_id=1, source_target_pairs={{1,0},{2,1},{3,2},{4,3},{5,4},{6,5},{7,6},{8,7},{9,8},{10,9},{11,1... | collective-permute-start | bytes 24584 | tf_op jit(solution)/shard_map/while/body/eval_jaxpr/ppermute | solution.py:14
  460.2 18.4 %collective-permute-start.1 = (bf16[2,1,32,64]{3,2,1,0:T(8,128)(2,1)S(1)}, bf16[2,1,32,64]{3,2,1,0:T(8,128)(2,1)S(1)}, u32[]{:S(2)}, u32[]{:S(2)}) collective-permute-start(bf16[2,1,32,64]{3,2,1,0:T(8,128)(2,1)S(1)} %get-tuple-element.187), channel_id=1, source_target_pairs={{0,1},{1,2},{2,3},{3,4},{4,5},{5,6},{6,7},{7,8},{8,9},{9,10},{10,1... | collective-permute-start | bytes 24584 | tf_op jit(solution)/shard_map/while/body/eval_jaxpr/ppermute | solution.py:13
  505.3 18.4 %collective-permute-start.1 = (bf16[2,1,32,64]{3,2,1,0:T(8,128)(2,1)S(1)}, bf16[2,1,32,64]{3,2,1,0:T(8,128)(2,1)S(1)}, u32[]{:S(2)}, u32[]{:S(2)}) collective-permute-start(bf16[2,1,32,64]{3,2,1,0:T(8,128)(2,1)S(1)} %get-tuple-element.187), channel_id=1, source_target_pairs={{0,1},{1,2},{2,3},{3,4},{4,5},{5,6},{6,7},{7,8},{8,9},{9,10},{10,1... | collective-permute-start | bytes 24584 | tf_op jit(solution)/shard_map/while/body/eval_jaxpr/ppermute | solution.py:13
  550.5 18.4 %collective-permute-start.1 = (bf16[2,1,32,64]{3,2,1,0:T(8,128)(2,1)S(1)}, bf16[2,1,32,64]{3,2,1,0:T(8,128)(2,1)S(1)}, u32[]{:S(2)}, u32[]{:S(2)}) collective-permute-start(bf16[2,1,32,64]{3,2,1,0:T(8,128)(2,1)S(1)} %get-tuple-element.187), channel_id=1, source_target_pairs={{0,1},{1,2},{2,3},{3,4},{4,5},{5,6},{6,7},{7,8},{8,9},{9,10},{10,1... | collective-permute-start | bytes 24584 | tf_op jit(solution)/shard_map/while/body/eval_jaxpr/ppermute | solution.py:13
  595.7 18.4 %collective-permute-start.1 = (bf16[2,1,32,64]{3,2,1,0:T(8,128)(2,1)S(1)}, bf16[2,1,32,64]{3,2,1,0:T(8,128)(2,1)S(1)}, u32[]{:S(2)}, u32[]{:S(2)}) collective-permute-start(bf16[2,1,32,64]{3,2,1,0:T(8,128)(2,1)S(1)} %get-tuple-element.187), channel_id=1, source_target_pairs={{0,1},{1,2},{2,3},{3,4},{4,5},{5,6},{6,7},{7,8},{8,9},{9,10},{10,1... | collective-permute-start | bytes 24584 | tf_op jit(solution)/shard_map/while/body/eval_jaxpr/ppermute | solution.py:13
  640.8 18.4 %collective-permute-start.1 = (bf16[2,1,32,64]{3,2,1,0:T(8,128)(2,1)S(1)}, bf16[2,1,32,64]{3,2,1,0:T(8,128)(2,1)S(1)}, u32[]{:S(2)}, u32[]{:S(2)}) collective-permute-start(bf16[2,1,32,64]{3,2,1,0:T(8,128)(2,1)S(1)} %get-tuple-element.187), channel_id=1, source_target_pairs={{0,1},{1,2},{2,3},{3,4},{4,5},{5,6},{6,7},{7,8},{8,9},{9,10},{10,1... | collective-permute-start | bytes 24584 | tf_op jit(solution)/shard_map/while/body/eval_jaxpr/ppermute | solution.py:13
  686.0 18.4 %collective-permute-start.1 = (bf16[2,1,32,64]{3,2,1,0:T(8,128)(2,1)S(1)}, bf16[2,1,32,64]{3,2,1,0:T(8,128)(2,1)S(1)}, u32[]{:S(2)}, u32[]{:S(2)}) collective-permute-start(bf16[2,1,32,64]{3,2,1,0:T(8,128)(2,1)S(1)} %get-tuple-element.187), channel_id=1, source_target_pairs={{0,1},{1,2},{2,3},{3,4},{4,5},{5,6},{6,7},{7,8},{8,9},{9,10},{10,1... | collective-permute-start | bytes 24584 | tf_op jit(solution)/shard_map/while/body/eval_jaxpr/ppermute | solution.py:13
  731.2 18.4 %collective-permute-start.1 = (bf16[2,1,32,64]{3,2,1,0:T(8,128)(2,1)S(1)}, bf16[2,1,32,64]{3,2,1,0:T(8,128)(2,1)S(1)}, u32[]{:S(2)}, u32[]{:S(2)}) collective-permute-start(bf16[2,1,32,64]{3,2,1,0:T(8,128)(2,1)S(1)} %get-tuple-element.187), channel_id=1, source_target_pairs={{0,1},{1,2},{2,3},{3,4},{4,5},{5,6},{6,7},{7,8},{8,9},{9,10},{10,1... | collective-permute-start | bytes 24584 | tf_op jit(solution)/shard_map/while/body/eval_jaxpr/ppermute | solution.py:13
  (63 other events, 387.3 us)
where the time goes:
time: 790 us; the launch traced here: 776 us
  local copies, waits for them, and re-layouts  268 us (34%)
  starting transfers between devices  253 us (32%)
  other arithmetic  166 us (21%)
  matrix products  82 us (10%)
    ppermute x34, starting transfers between devices, edge_swap(): from_next = lax.ppermute(low_edge, axis_label, up_pairs)  198 us
    concatenate x32, local copies, waits for them, and re-layouts, conv_taps(): patches = jnp.concatenate(tap_list, axis=-1)  169 us
    concatenate x33, other arithmetic, edge_swap(): return jnp.concatenate([from_prev, tile_arr, from_next], axis=split_dim)  111 us
    dot_general x32, matrix products, conv_taps(): jnp.dot(flat_patches, flat_weights, preferred_element_type=jnp.float32)  82 us
    dynamic_update_slice x16, other arithmetic, local_run(): final_pair, all_hidden = lax.scan(step_fn, (h_init, c_init), frames_ext)  55.6 us
    ppermute x34, starting transfers between devices, edge_swap(): from_prev = lax.ppermute(high_edge, axis_label, down_pairs)  55.6 us
    slice x16, local copies, waits for them, and re-layouts, conv_taps(): padded[:, row_off:row_off + out_rows, col_off:col_off + out_cols, :]  37.9 us
    unnamed x11, local copies, waits for them, and re-layouts  19.7 us
  transfers between devices with their start and end apart: 68, of which 2 were waited for; matrix products, arithmetic and copies ran while one was open for 25% of the time, Pallas kernels for 0%

commit v1 on v0

v1 whole, which is shorter than its diff:
```python
import functools

import jax
import jax.numpy as jnp
from jax import lax
from jax.experimental import pallas as pl
from jax.experimental.pallas import tpu as pltpu
from jax.sharding import PartitionSpec as P

MESH = pl.DeviceIdType.MESH
CH = 64
LANES = 128
PIECE = 4
RING = 8


def cuts(lo, hi):
    n = max(1, (hi - lo) // PIECE)
    edges = [lo + i * PIECE for i in range(n)] + [hi]
    return list(zip(edges[:-1], edges[1:]))


def kernel(T, K, R, W, n_rows, frames, w_x, w_h, bias, h_init, c_init, h_out, c_out,
           xin, hout, cst, hst, xh_even, xh_odd, cbuf, shift, wbuf,
           xs_ref, xr_ref, hs_ref, hr_ref, cs_ref, cr_ref,
           s_w, s_x, s_xr, s_xs, s_i, s_ir, s_is, s_hx, s_hxs, s_hh, s_hhs, s_hc, s_hcs,
           s_o, s_os, s_or):
    s = lax.axis_index("cols")
    n = lax.axis_index("rows")
    p = 1 - s
    HW = W // 2
    NB = T // K
    per_block = K * (K + 1) // 2
    off = [sum(K - i for i in range(o)) for o in range(K)]
    mine = pl.ds(pl.multiple_of(s * HW, HW), HW)
    theirs = pl.ds(pl.multiple_of(p * HW, HW), HW)
    has_up, has_dn = n > 0, n < n_rows - 1

    def local(src, dst, sem):
        return pltpu.make_async_copy(src, dst, sem)

    def remote(src, dst, ssem, rsem, dev):
        return pltpu.make_async_remote_copy(
            src_ref=src, dst_ref=dst, send_sem=ssem, recv_sem=rsem, device_id=dev, device_id_type=MESH)

    peer = {"cols": p}
    side_dev = [{"rows": n - 1}, {"rows": n + 1}]
    side_ok = [has_up, has_dn]

    local(w_h, wbuf.at[:, :, 0], s_w.at[0]).start()
    local(w_x, wbuf.at[:, :, 1], s_w.at[1]).start()
    local(h_init.at[s], hst.at[:, mine], s_i.at[0]).start()
    local(c_init.at[s], cst.at[:, mine], s_i.at[1]).start()

    def own_x(t, _):
        local(frames.at[t, s], xin.at[t, :, mine], s_x.at[t]).start()
        return 0

    lax.fori_loop(0, T, own_x, 0)

    barrier = pltpu.get_barrier_semaphore()
    pl.semaphore_signal(barrier, inc=1, device_id=peer, device_id_type=MESH)
    for ok, dev in zip(side_ok, side_dev):
        @pl.when(ok)
        def _():
            pl.semaphore_signal(barrier, inc=1, device_id=dev, device_id_type=MESH)
    pl.semaphore_wait(barrier, 1 + has_up.astype(jnp.int32) + has_dn.astype(jnp.int32))

    h_push = remote(h_init.at[p], hst.at[:, mine], s_is.at[0], s_ir.at[0], peer)
    c_push = remote(c_init.at[p], cst.at[:, mine], s_is.at[1], s_ir.at[1], peer)
    h_push.start()

    def push_x(t, _):
        remote(frames.at[t, p], xin.at[t, :, mine], s_xs, s_xr.at[t], peer).start()
        return 0

    push_x(0, 0)
    c_push.start()
    lax.fori_loop(1, T, push_x, 0)

    shift[...] = jnp.zeros_like(shift)
    lane = lax.broadcasted_iota(jnp.int32, (W, LANES), 1)
    low = lane < CH
    low_half = lane[: HW] < CH
    low_row = lax.broadcasted_iota(jnp.int32, (1, LANES), 1) < CH
    scale = jnp.where(low_row, 0.5, 1.0)
    shiftup = jnp.where(low_row, 0.5, 0.0)

    local(w_h, wbuf.at[:, :, 0], s_w.at[0]).wait()
    local(w_x, wbuf.at[:, :, 1], s_w.at[1]).wait()
    for dr in range(3):
        for dc in range(3):
            for half in range(2):
                tile = wbuf[dr, dc, half, :, 0:LANES]
                wbuf[dr, dc, half, :, 0:LANES] = jnp.concatenate([tile[:, CH:], tile[:, :CH]], axis=1)
    b_first = bias[:, 0:LANES]
    b_fi = jnp.concatenate([b_first[:, CH:], b_first[:, :CH]], axis=1) * 0.5
    b_og = bias[:, LANES:] * scale

    def wait_x(t):
        local(frames.at[t, s], xin.at[t, :, mine], s_x.at[t]).wait()
        local(frames.at[t, s], xin.at[t, :, theirs], s_xr.at[t]).wait()

    def emit(nxt, r, hx):
        slot = (r + K) % RING
        row = r + K
        shift[slot, 8:8 + W, :] = hx
        nxt[1, row] = hx.astype(jnp.bfloat16)
        nxt[0, row] = shift[slot, 7:7 + W, :].astype(jnp.bfloat16)
        nxt[2, row] = shift[slot, 9:9 + W, :].astype(jnp.bfloat16)

    def x_row(t, b, o, r):
        if 0 <= r < R:
            return xin[t, r].astype(jnp.float32)
        side, i = (0, r + (K - o)) if r < 0 else (1, r - R)
        packed = xr_ref[side, b * per_block + off[o] + i].astype(jnp.float32)
        return jnp.concatenate([packed[:, :CH], packed[:, CH:]], axis=0)

    def masked(r, v):
        if r < 0:
            return jnp.where(has_up, v, 0.0)
        if r >= R:
            return jnp.where(has_dn, v, 0.0)
        return v

    def pack(v):
        return jnp.concatenate([v[:HW], v[HW:]], axis=1)

    def send_x(t, b, o):
        for side in range(2):
            lo = b * per_block + off[o]
            for i in range(K - o):
                r = i if side == 0 else R - (K - o) + i
                xs_ref[side, lo + i] = pack(xin[t, r])

    def copy_x(b, o, side):
        rows = pl.ds(b * per_block + off[o], K - o)
        return remote(xs_ref.at[side, rows], xr_ref.at[1 - side, rows], s_hxs.at[side],
                      s_hx.at[1 - side, b * K + o], side_dev[side])

    def start_x(b, o):
        for side in range(2):
            @pl.when(side_ok[side])
            def _():
                copy_x(b, o, side).start()

    def send_state(b, h_rows):
        for side in range(2):
            for i in range(K):
                r = i if side == 0 else R - K + i
                hs_ref[side, b * K + i] = pack(h_rows[r])
            for i in range(K - 1):
                r = i if side == 0 else R - (K - 1) + i
                c = cbuf[r + K]
                cs_ref[side, b * (K - 1) + i] = jnp.where(low_half, c[:HW], c[HW:])

    def copy_h(b, side):
        rows = pl.ds(b * K, K)
        return remote(hs_ref.at[side, rows], hr_ref.at[1 - side, rows], s_hhs.at[side, b],
                      s_hh.at[1 - side, b], side_dev[side])

    def copy_c(b, side):
        rows = pl.ds(b * (K - 1), K - 1)
        return remote(cs_ref.at[side, rows], cr_ref.at[1 - side, rows], s_hcs.at[side, b],
                      s_hc.at[1 - side, b], side_dev[side])

    def start_state(b):
        for side in range(2):
            @pl.when(side_ok[side])
            def _():
                copy_h(b, side).start()
                copy_c(b, side).start()

    wait_x(0)
    local(h_init.at[s], hst.at[:, mine], s_i.at[0]).wait()
    h_push.wait_recv()
    local(c_init.at[s], cst.at[:, mine], s_i.at[1]).wait()
    c_push.wait_recv()
    for r in range(R):
        c = cst[r]
        cbuf[r + K] = jnp.concatenate([c, c], axis=1)
    send_state(0, hst)
    send_x(0, 0, 0)
    start_state(0)
    start_x(0, 0)
    for r in range(R):
        emit(xh_even, r, jnp.concatenate([hst[r].astype(jnp.float32), x_row(0, 0, 0, r)], axis=1))

    weights = wbuf[...].reshape(9 * LANES, 4 * CH)

    def piece(b, o, lo, hi):
        cur, nxt = (xh_even, xh_odd) if o % 2 == 0 else (xh_odd, xh_even)
        t = b * K + o
        t_next = jnp.minimum(t + 1, T - 1)
        b_next, o_next = (b, o + 1) if o + 1 < K else (b + 1, 0)
        m = hi - lo
        taps = [cur[dc, lo + K + dr - 1:hi + K + dr - 1].reshape(m * W, LANES) for dr in range(3) for dc in range(3)]
        gates = jnp.dot(jnp.concatenate(taps, axis=1), weights, preferred_element_type=jnp.float32)
        for q in range(m):
            r = lo + q
            g = gates[q * W:(q + 1) * W]
            fi = jnp.tanh(g[:, :LANES] * 0.5 + b_fi) * 0.5 + 0.5
            og = jnp.tanh(g[:, LANES:] * scale + b_og) * scale + shiftup
            prod = fi * jnp.where(low, cbuf[r + K], og)
            c = prod + pltpu.roll(prod, CH, 1)
            cbuf[r + K] = c
            h = masked(r, og * jnp.tanh(c))
            if 0 <= r < R:
                hout[t, r] = h[:, :CH].astype(jnp.bfloat16)
            x = masked(r, x_row(t_next, b_next, o_next, r))
            emit(nxt, r, jnp.concatenate([h[:, :CH], x], axis=1))

    def out_own(t):
        return local(hout.at[t, :, mine], h_out.at[t, s], s_o)

    def out_peer(t):
        return remote(hout.at[t, :, theirs], h_out.at[t, s], s_os, s_or, peer)

    def block(b, _):
        more = b + 1 < NB
        for o in range(K):
            t = b * K + o
            if o + 1 < K:
                wait_x(t + 1)
                send_x(t + 1, b, o + 1)
                start_x(b, o + 1)
            else:
                @pl.when(more)
                def _():
                    wait_x(t + 1)
                    send_x(t + 1, b + 1, 0)
                    start_x(b + 1, 0)
            for lo, hi in cuts(o + 1, R - 1 - o):
                piece(b, o, lo, hi)
        for side in range(2):
            @pl.when(side_ok[side])
            def _():
                copy_h(b, 1 - side).wait_recv()
                copy_c(b, 1 - side).wait_recv()
                copy_x(b, 0, 1 - side).wait_recv()
        for side in range(2):
            for i in range(K):
                r = i - K if side == 0 else R + i
                packed = hr_ref[side, b * K + i].astype(jnp.float32)
                h = jnp.concatenate([packed[:, :CH], packed[:, CH:]], axis=0)
                hx = jnp.concatenate([h, x_row(b * K, b, 0, r)], axis=1)
                emit(xh_even, r, masked(r, hx))
            for i in range(K - 1):
                r = i - (K - 1) if side == 0 else R + i
                packed = cr_ref[side, b * (K - 1) + i]
                cbuf[r + K, 0:HW] = packed
                cbuf[r + K, HW:W] = pltpu.roll(packed, CH, 1)
        for o in range(K):
            if o + 1 < K:
                for side in range(2):
                    @pl.when(side_ok[side])
                    def _():
                        copy_x(b, o + 1, 1 - side).wait_recv()
            m = K - 1 - o
            for (a, e), (a2, e2) in zip(cuts(-m, o + 1), cuts(R - 1 - o, R + m)):
                piece(b, o, a, e)
                piece(b, o, a2, e2)
            out_own(b * K + o).start()
            out_peer(b * K + o).start()

        @pl.when(more)
        def _():
            send_state(b + 1, hout.at[b * K + K - 1])
            start_state(b + 1)
        return 0

    lax.fori_loop(0, NB, block, 0)

    for r in range(R):
        cst[r] = cbuf[r + K, :, 0:CH]
    c_own = local(cst.at[:, mine], c_out.at[s], s_i.at[0])
    c_peer = remote(cst.at[:, theirs], c_out.at[s], s_is.at[2], s_ir.at[2], peer)
    c_own.start()
    c_peer.start()

    h_push.wait_send()
    c_push.wait_send()
    local(xin.at[:, :, mine], xin.at[:, :, mine], s_xs).wait()
    for side in range(2):
        @pl.when(side_ok[side])
        def _():
            local(xs_ref.at[side], xs_ref.at[side], s_hxs.at[side]).wait()
            for b in range(NB):
                copy_h(b, side).wait_send()
                copy_c(b, side).wait_send()
    local(hout.at[:, :, mine], hout.at[:, :, mine], s_o).wait()
    local(hout.at[:, :, mine], hout.at[:, :, mine], s_os).wait()
    local(hout.at[:, :, mine], hout.at[:, :, mine], s_or).wait()
    c_own.wait()
    c_peer.wait()


def run(K, n_rows, frames, w_x, w_h, gate_bias, h_init, c_init):
    T, S, R, HW = frames.shape[:4]
    W = 2 * HW
    NB = T // K
    per_block = K * (K + 1) // 2
    bf, f32 = jnp.bfloat16, jnp.float32
    vm, dma = pltpu.VMEM, pltpu.SemaphoreType.DMA
    hbm = pl.BlockSpec(memory_space=pltpu.HBM)
    return pl.pallas_call(
        functools.partial(kernel, T, K, R, W, n_rows),
        out_shape=(jax.ShapeDtypeStruct(frames.shape, bf), jax.ShapeDtypeStruct(c_init.shape, f32)),
        in_specs=[hbm, hbm, hbm, pl.BlockSpec(memory_space=pltpu.VMEM), hbm, hbm],
        out_specs=(hbm, hbm),
        scratch_shapes=[
            vm((T, R, W, CH), bf), vm((T, R, W, CH), bf), vm((R, W, CH), f32), vm((R, W, CH), bf),
            vm((3, R + 2 * K, W, LANES), bf), vm((3, R + 2 * K, W, LANES), bf),
            vm((R + 2 * K, W, LANES), f32), vm((RING, W + 16, LANES), f32), vm((3, 3, 2, CH, 4 * CH), bf),
            vm((2, NB * per_block, HW, LANES), bf), vm((2, NB * per_block, HW, LANES), bf),
            vm((2, NB * K, HW, LANES), bf), vm((2, NB * K, HW, LANES), bf),
            vm((2, NB * (K - 1), HW, LANES), f32), vm((2, NB * (K - 1), HW, LANES), f32),
            dma((2,)), dma((T,)), dma((T,)), dma, dma((2,)), dma((3,)), dma((3,)),
            dma((2, T)), dma((2,)), dma((2, NB)), dma((2, NB)), dma((2, NB)), dma((2, NB)),
            dma, dma, dma],
        compiler_params=pltpu.CompilerParams(collective_id=0, has_side_effects=True, vmem_limit_bytes=62 * 2**20),
    )(frames, w_x, w_h, gate_bias.reshape(1, -1), h_init, c_init)


def solution(mesh, K=4):
    n_rows = mesh.shape["rows"]
    frame_spec = P(None, "batch", "rows", "cols", None)
    state_spec = P("batch", "rows", "cols", None)
    return jax.shard_map(functools.partial(run, K, n_rows), mesh=mesh,
                         in_specs=(frame_spec, P(), P(), P(), state_spec, state_spec),
                         out_specs=(frame_spec, state_spec), check_vma=False)
```

time: 790 us -> 62.3 us (0.08); the launches traced: 776 us -> 62.2 us
  local copies, waits for them, and re-layouts: 268 us -> 10.2 us
  starting transfers between devices: 253 us -> 0 us
  other arithmetic: 166 us -> 0 us
  matrix products: 82 us -> 0 us
  Pallas kernels: 0 us -> 51.4 us
    ppermute x68 -> x0, starting transfers between devices: 253 us -> none  [the longest x34 198 us: edge_swap(): from_next = lax.ppermute(low_edge, axis_label, up_pairs)]
    concatenate x49 -> x0, local copies, waits for them, and re-layouts: 170 us -> none  [the longest x32 169 us: conv_taps(): patches = jnp.concatenate(tap_list, axis=-1)]
    concatenate x33 -> x0, other arithmetic: 111 us -> none  [edge_swap(): return jnp.concatenate([from_prev, tile_arr, from_next], axis=split_dim)]
    dot_general x32 -> x0, matrix products: 82 us -> none  [conv_taps(): jnp.dot(flat_patches, flat_weights, preferred_element_type=jnp.float32)]
    dynamic_update_slice x16 -> x0, other arithmetic: 55.6 us -> none  [local_run(): final_pair, all_hidden = lax.scan(step_fn, (h_init, c_init), frames_ext)]
    pallas_call x0 -> x1, Pallas kernels: none -> 51.4 us  [run(): pl.pallas_call(functools.partial(kernel, T, K, R, W, n_rows), out_shape=(...]
    slice x50 -> x0, local copies, waits for them, and re-layouts: 41.2 us -> none  [the longest x16 37.9 us: conv_taps(): padded[:, row_off:row_off + out_rows, col_off:col_off + out_cols, :]]
    squeeze x16 -> x0, local copies, waits for them, and re-layouts: 18.7 us -> none  [local_run(): final_pair, all_hidden = lax.scan(step_fn, (h_init, c_init), frames_ext)]
  transfers between devices with their start and end apart: 68 -> 0, of which waited for: 2 -> 0; matrix products, arithmetic and copies ran while one was open for 25% -> 0% of each run, Pallas kernels for 0% -> 0%
where the time goes in v1:
time: 62.3 us; the launch traced here: 62.2 us
  Pallas kernels  51.4 us (83%)
  local copies, waits for them, and re-layouts  10.2 us (16%)
  between operations  0.65 us (1%)
    pallas_call x1, Pallas kernels, run(): pl.pallas_call(functools.partial(kernel, T, K, R, W, n_rows), out_shape=(...  51.4 us
    unnamed x4, local copies, waits for them, and re-layouts  10.2 us

profile of v1, /device:TPU:97, one launch (start us, length us, event | category | flops | bytes accessed | tf_op | source)
XLA Modules:
  0.0 62.2 jit_solution(8239379627092525095)
XLA Ops:
  0.6 51.4 %shard_map.77 = (bf16[16,2,32,32,64]{4,3,2,1,0:T(8,128)(2,1)}, f32[2,32,32,64]{3,2,1,0:T(8,128)}) custom-call(bf16[16,2,32,32,64]{4,3,2,1,0:T(8,128)(2,1)} %frames.1, bf16[3,3,64,256]{3,2,1,0:T(8,128)(2,1)} %w_x.1, bf16[3,3,64,256]{3,2,1,0:T(8,128)(2,1)} %w_h.1, f32[1,256]{1,0:T(1,128)} %bitcast.1, bf16[2,32,32,64]{3,2,1,0:T(8,128)(2,1)} %h_init.1, ...), custom_call_target="tpu_custom_call" | custom-call | tf_op jit(solution)/shard_map/pallas_call | solution.py:306
  52.0 0.0 copy-start
  52.0 9.2 %copy.10 = bf16[16,2,32,32,64]{4,3,2,1,0:T(8,128)(2,1)} copy(bf16[16,2,32,32,64]{4,3,2,1,0:T(8,128)(2,1)} %get-tuple-element.4) | data formatting | bytes 8388608
  61.2 0.0 copy-done
  61.2 1.0 %copy.11 = f32[2,32,32,64]{3,2,1,0:T(8,128)} copy(f32[2,32,32,64]{3,2,1,0:T(8,128)S(1)} %copy-done) | data formatting | bytes 1048576
Async XLA Ops:
  52.0 9.2 %copy-start = (f32[2,32,32,64]{3,2,1,0:T(8,128)S(1)}, f32[2,32,32,64]{3,2,1,0:T(8,128)}, u32[]{:S(2)}) copy-start(f32[2,32,32,64]{3,2,1,0:T(8,128)} %get-tuple-element.5) | copy-start | bytes 1572868

commit v2 on v0

v2 whole, which is shorter than its diff:
```python
import functools

import jax
import jax.numpy as jnp
from jax import lax
from jax.experimental import pallas as pl
from jax.experimental.pallas import tpu as pltpu
from jax.sharding import PartitionSpec as P

MESH = pl.DeviceIdType.MESH
CH = 64
LANES = 128
PIECE = 4
RING = 8
BLOCKS = (4, 4, 4, 4)


def cuts(lo, hi, size=PIECE):
    n = max(1, (hi - lo) // size)
    edges = [lo + i * size for i in range(n)] + [hi]
    return list(zip(edges[:-1], edges[1:]))


class Plan:
    def __init__(self, blocks, T, R, W):
        assert sum(blocks) == T
        self.blocks, self.T, self.R, self.W, self.HW = blocks, T, R, W, W // 2
        self.K = max(blocks)
        self.first = [sum(blocks[:b]) for b in range(len(blocks))]
        self.of = [(b, o) for b, k in enumerate(blocks) for o in range(k)]
        self.xrows = [blocks[b] - o for b, o in self.of]
        self.xat = [sum(self.xrows[:t]) for t in range(T + 1)]
        self.hat = [sum(blocks[:b]) for b in range(len(blocks) + 1)]
        self.cat = [sum(k - 1 for k in blocks[:b]) for b in range(len(blocks) + 1)]
        ends = [0, 1] + [min(f + k + 1, T) for f, k in zip(self.first, blocks)]
        self.groups = [(a, e) for a, e in zip(ends[:-1], ends[1:]) if e > a]


def kernel(plan, n_rows, frames, w_x, w_h, bias, h_init, c_init, hout, hpeer, cout, cpeer,
           xin, hst, cst, xh_even, xh_odd, cbuf, shift, wbuf,
           xs_ref, xr_ref, hs_ref, hr_ref, cs_ref, cr_ref,
           s_w, s_i, s_ir, s_is, s_x, s_xr, s_xs, s_b, s_bs, s_or, s_os, s_c):
    T, R, W, HW = plan.T, plan.R, plan.W, plan.HW
    PAD = plan.K
    NB = len(plan.blocks)
    s = lax.axis_index("cols")
    n = lax.axis_index("rows")
    p = 1 - s
    mine = pl.ds(pl.multiple_of(s * HW, HW), HW)
    theirs = pl.ds(pl.multiple_of(p * HW, HW), HW)
    has_up, has_dn = n > 0, n < n_rows - 1
    bf, f32 = jnp.bfloat16, jnp.float32

    def local(src, dst, sem):
        return pltpu.make_async_copy(src, dst, sem)

    def remote(src, dst, ssem, rsem, dev):
        return pltpu.make_async_remote_copy(
            src_ref=src, dst_ref=dst, send_sem=ssem, recv_sem=rsem, device_id=dev, device_id_type=MESH)

    peer = {"cols": p}
    side_dev = [{"rows": lax.rem(n + n_rows - 1, n_rows)}, {"rows": lax.rem(n + 1, n_rows)}]

    w_copies = [local(w_h, wbuf.at[:, :, 0], s_w.at[0]), local(w_x, wbuf.at[:, :, 1], s_w.at[1])]
    h_own = local(h_init.at[s], hst.at[:, mine], s_i.at[0])
    c_own = local(c_init.at[s], cst.at[:, mine], s_i.at[1])
    x_own = [local(frames.at[a:e, s], xin.at[a:e, :, mine], s_x.at[g]) for g, (a, e) in enumerate(plan.groups)]
    for c in [h_own, c_own, x_own[0], *w_copies, *x_own[1:]]:
        c.start()

    barrier = pltpu.get_barrier_semaphore()
    for dev in [peer, *side_dev]:
        pl.semaphore_signal(barrier, inc=1, device_id=dev, device_id_type=MESH)
    pl.semaphore_wait(barrier, 3)

    h_push = remote(h_init.at[p], hst.at[:, mine], s_is.at[0], s_ir.at[0], peer)
    c_push = remote(c_init.at[p], cst.at[:, mine], s_is.at[1], s_ir.at[1], peer)
    x_push = [remote(frames.at[a:e, p], xin.at[a:e, :, mine], s_xs.at[g], s_xr.at[g], peer)
              for g, (a, e) in enumerate(plan.groups)]
    for c in [h_push, c_push, *x_push]:
        c.start()

    shift[...] = jnp.zeros_like(shift)
    low = lax.broadcasted_iota(jnp.int32, (1, LANES), 1) < CH
    low_half = low_row = low
    turn = [0]
    scale = jnp.where(low_row, 0.5, 1.0)
    lift = jnp.where(low_row, 0.5, 0.0)

    for c in w_copies:
        c.wait()
    for dr in range(3):
        for dc in range(3):
            for half in range(2):
                tile = wbuf[dr, dc, half, :, 0:LANES]
                wbuf[dr, dc, half, :, 0:LANES] = jnp.concatenate([tile[:, CH:], tile[:, :CH]], axis=1)
    b_first = bias[:, 0:LANES]
    b_fi = jnp.concatenate([b_first[:, CH:], b_first[:, :CH]], axis=1) * 0.5
    b_og = bias[:, LANES:] * scale

    def pack(v):
        return jnp.concatenate([v[:, :HW], v[:, HW:]], axis=2)

    def unpack(v):
        return jnp.concatenate([v[:, :, :CH], v[:, :, CH:]], axis=1)

    def masked(r, v):
        if r < 0:
            return jnp.where(has_up, v, 0.0)
        if r >= R:
            return jnp.where(has_dn, v, 0.0)
        return v

    def emit(t, lo, hi, hx):
        nxt = xh_even if t % 2 == 0 else xh_odd
        at, to = slot(lo, hi), slice(lo + PAD, hi + PAD)
        shift[at, 8:8 + W, :] = hx
        nxt[1, to] = hx.astype(bf)
        nxt[0, to] = shift[at, 7:7 + W, :].astype(bf)
        nxt[2, to] = shift[at, 9:9 + W, :].astype(bf)

    def slot(lo, hi):
        if turn[0] + hi - lo > RING:
            turn[0] = 0
        turn[0] += hi - lo
        return slice(turn[0] - (hi - lo), turn[0])

    def x_rows(t, lo, hi):
        if lo >= 0 and hi <= R:
            return xin[t, lo:hi].astype(f32)
        side, i = (0, lo + plan.xrows[t]) if lo < 0 else (1, lo - R)
        return unpack(xr_ref[side, plan.xat[t] + i:plan.xat[t] + i + hi - lo].astype(f32))

    def wait_x(g):
        if g < len(plan.groups):
            x_own[g].wait()
            x_push[g].wait_recv()

    def border(b, kind, side):
        k, f = plan.blocks[b], plan.first[b]
        src, dst, at, count = [
            (xs_ref, xr_ref, plan.xat[f], plan.xat[f + k] - plan.xat[f]),
            (hs_ref, hr_ref, plan.hat[b], k),
            (cs_ref, cr_ref, plan.cat[b], k - 1)][kind]
        return remote(src.at[side, at:at + count], dst.at[1 - side, at:at + count],
                      s_bs.at[kind, side, b], s_b.at[kind, 1 - side, b], side_dev[side])

    def send_x(b):
        k, f = plan.blocks[b], plan.first[b]
        for side in range(2):
            for t in range(f, f + k):
                m = plan.xrows[t]
                lo = 0 if side == 0 else R - m
                xs_ref[side, plan.xat[t]:plan.xat[t] + m] = pack(xin[t, lo:lo + m])
            border(b, 0, side).start()

    def send_state(b, h_rows):
        k = plan.blocks[b]
        for side in range(2):
            lo = 0 if side == 0 else R - k
            hs_ref[side, plan.hat[b]:plan.hat[b] + k] = pack(h_rows[lo:lo + k])
            lo = PAD if side == 0 else PAD + R - (k - 1)
            c = cbuf[lo:lo + k - 1]
            cs_ref[side, plan.cat[b]:plan.cat[b] + k - 1] = jnp.where(low_half, c[:, :HW], c[:, HW:])
        for side in range(2):
            border(b, 1, side).start()
            border(b, 2, side).start()

    weights = wbuf[...].reshape(9 * LANES, 4 * CH)

    def dot(t, lo, hi):
        cur = xh_even if t % 2 == 0 else xh_odd
        taps = [cur[dc, lo + PAD + dr - 1:hi + PAD + dr - 1].reshape((hi - lo) * W, LANES)
                for dr in range(3) for dc in range(3)]
        return jnp.dot(jnp.concatenate(taps, axis=1), weights, preferred_element_type=f32)

    def cells(t, lo, hi, gates):
        m, g = hi - lo, gates
        fi = jnp.tanh(g[:, :LANES] * 0.5 + b_fi) * 0.5 + 0.5
        og = jnp.tanh(g[:, LANES:] * scale + b_og) * scale + lift
        prod = fi * jnp.where(low, cbuf[lo + PAD:hi + PAD].reshape(m * W, LANES), og)
        c = prod + pltpu.roll(prod, CH, 1)
        h = (og * jnp.tanh(c)).reshape(m, W, LANES)
        c = c.reshape(m, W, LANES)
        if t == T - 1:
            cout[lo:hi] = c[:, :, :CH]
        else:
            cbuf[lo + PAD:hi + PAD] = c
        for a, e in ((lo, min(hi, 0)), (max(lo, 0), min(hi, R)), (max(lo, R), hi)):
            if a >= e:
                continue
            part = h[a - lo:e - lo, :, :CH]
            if a >= 0 and e <= R:
                hout[t, a:e] = part.astype(bf)
            if t < T - 1:
                emit(t + 1, a, e, masked(a, jnp.concatenate([part, x_rows(t + 1, a, e)], axis=2)))

    pending = []

    def piece(t, lo, hi):
        gates = dot(t, lo, hi)
        flush()
        pending.append((t, lo, hi, gates))

    def flush():
        while pending:
            cells(*pending.pop())

    def out_peer(t0, t1, g):
        return remote(hout.at[t0:t1, :, theirs], hpeer.at[t0:t1], s_os.at[g], s_or.at[g], peer)

    h_own.wait()
    h_push.wait_recv()
    c_own.wait()
    c_push.wait_recv()
    c0 = cst[...]
    cbuf[PAD:PAD + R] = jnp.concatenate([c0, c0], axis=2)
    send_state(0, hst)
    wait_x(0)
    wait_x(1)
    send_x(0)
    for lo, hi in cuts(0, R):
        emit(0, lo, hi, jnp.concatenate([hst[lo:hi].astype(f32), x_rows(0, lo, hi)], axis=2))

    outs = []
    for b, k in enumerate(plan.blocks):
        f = plan.first[b]
        for o in range(k):
            t = f + o
            if o == 0:
                inner = [(1, k + 1), *cuts(k + 1, R - 1 - k), (R - 1 - k, R - 1)]
            else:
                inner = cuts(o + 1, R - 1 - o)
            for i, (lo, hi) in enumerate(inner[1:-1] + [inner[0], inner[-1]]):
                piece(t, lo, hi)
                if b and o == 0 and i == 0:
                    send_state(b, hout.at[f - 1])
                    outs.append(out_peer(plan.first[b - 1], f, b - 1))
                    outs[-1].start()
        for kind in (1, 2, 0):
            for side in range(2):
                border(b, kind, side).wait_recv()
        wait_x(b + 2)
        for side in range(2):
            lo = -k if side == 0 else R
            h = unpack(hr_ref[side, plan.hat[b]:plan.hat[b] + k].astype(f32))
            emit(f, lo, lo + k, masked(lo, jnp.concatenate([h, x_rows(f, lo, lo + k)], axis=2)))
            lo = PAD - (k - 1) if side == 0 else PAD + R
            packed = cr_ref[side, plan.cat[b]:plan.cat[b] + k - 1]
            cbuf[lo:lo + k - 1, 0:HW] = packed
            cbuf[lo:lo + k - 1, HW:W] = pltpu.roll(packed, CH, 2)
        if b + 1 < NB:
            send_x(b + 1)
        for o in range(k):
            m = k - 1 - o
            for (a, e), (a2, e2) in zip(cuts(-m, o + 1, max(PIECE, k)), cuts(R - 1 - o, R + m, max(PIECE, k))):
                piece(f + o, a, e)
                piece(f + o, a2, e2)
    flush()
    outs.append(out_peer(plan.first[-1], T, NB - 1))
    outs[-1].start()
    c_out = remote(cout.at[:, theirs], cpeer, s_c.at[0], s_c.at[1], peer)
    c_out.start()

    for c in [h_push, c_push, *x_push]:
        c.wait_send()
    for b in range(NB):
        for kind in range(3):
            for side in range(2):
                border(b, kind, side).wait_send()
    for c in [*outs, c_out]:
        c.wait()


def store(hout, hpeer, cout, cpeer, h_all, c_final, sems):
    s = lax.axis_index("cols")
    HW = hpeer.shape[2]
    mine = pl.ds(pl.multiple_of(s * HW, HW), HW)
    copies = [pltpu.make_async_copy(hout.at[:, :, mine], h_all.at[:, s], sems.at[0]),
              pltpu.make_async_copy(hpeer, h_all.at[:, 1 - s], sems.at[1]),
              pltpu.make_async_copy(cout.at[:, mine], c_final.at[s], sems.at[2]),
              pltpu.make_async_copy(cpeer, c_final.at[1 - s], sems.at[3])]
    for c in copies:
        c.start()
    for c in copies:
        c.wait()


def run(blocks, n_rows, frames, w_x, w_h, gate_bias, h_init, c_init):
    T, S, R, HW = frames.shape[:4]
    W = 2 * HW
    plan = Plan(blocks, T, R, W)
    NB, PAD, G = len(blocks), plan.K, len(plan.groups)
    bf, f32 = jnp.bfloat16, jnp.float32
    vm, dma = pltpu.VMEM, pltpu.SemaphoreType.DMA
    hbm = pl.BlockSpec(memory_space=pltpu.HBM)
    vmem = pl.BlockSpec(memory_space=pltpu.VMEM)
    parts = pl.pallas_call(
        functools.partial(kernel, plan, n_rows),
        out_shape=(vm((T, R, W, CH), bf), vm((T, R, HW, CH), bf), vm((R, W, CH), f32), vm((R, HW, CH), f32)),
        in_specs=[hbm, hbm, hbm, vmem, hbm, hbm],
        out_specs=(vmem,) * 4,
        scratch_shapes=[
            vm((T, R, W, CH), bf), vm((R, W, CH), bf), vm((R, W, CH), f32),
            vm((3, R + 2 * PAD, W, LANES), bf), vm((3, R + 2 * PAD, W, LANES), bf),
            vm((R + 2 * PAD, W, LANES), f32), vm((RING, W + 16, LANES), f32), vm((3, 3, 2, CH, 4 * CH), bf),
            vm((2, plan.xat[-1], HW, LANES), bf), vm((2, plan.xat[-1], HW, LANES), bf),
            vm((2, plan.hat[-1], HW, LANES), bf), vm((2, plan.hat[-1], HW, LANES), bf),
            vm((2, plan.cat[-1], HW, LANES), f32), vm((2, plan.cat[-1], HW, LANES), f32),
            dma((2,)), dma((2,)), dma((2,)), dma((2,)), dma((G,)), dma((G,)), dma((G,)),
            dma((3, 2, NB)), dma((3, 2, NB)), dma((NB,)), dma((NB,)), dma((2,))],
        compiler_params=pltpu.CompilerParams(collective_id=0, has_side_effects=True, vmem_limit_bytes=46 * 2**20),
    )(frames, w_x, w_h, gate_bias.reshape(1, -1), h_init, c_init)
    return pl.pallas_call(
        store,
        out_shape=(jax.ShapeDtypeStruct(frames.shape, bf), jax.ShapeDtypeStruct(c_init.shape, f32)),
        in_specs=[vmem] * 4,
        out_specs=(hbm, hbm),
        scratch_shapes=[dma((4,))],
        compiler_params=pltpu.CompilerParams(vmem_limit_bytes=2**20),
    )(*[pltpu.with_memory_space_constraint(a, pltpu.VMEM) for a in parts])


def solution(mesh, K=None):
    n_rows = mesh.shape["rows"]
    frame_spec = P(None, "batch", "rows", "cols", None)
    state_spec = P("batch", "rows", "cols", None)
    blocks = BLOCKS if K is None else K
    return jax.shard_map(functools.partial(run, blocks, n_rows), mesh=mesh,
                         in_specs=(frame_spec, P(), P(), P(), state_spec, state_spec),
                         out_specs=(frame_spec, state_spec), check_vma=False)
```

time: 790 us -> 59.6 us (0.08)
  the two profiles are of different devices: /device:TPU:97 before, /device:TPU:1 now
where the time goes in v2:
time: 59.6 us; the launch traced here: 59.5 us
  Pallas kernels  58.6 us (98%)
  between operations  0.82 us (1%)
    pallas_call x1, Pallas kernels, run(): pl.pallas_call(functools.partial(kernel, plan, n_rows), out_shape=(vm((T,...  55 us
    pallas_call x1, Pallas kernels, run(): pl.pallas_call(store, out_shape=(jax.ShapeDtypeStruct(frames.shape, bf),...  3.64 us

profile of v2, /device:TPU:1, one launch (start us, length us, event | category | flops | bytes accessed | tf_op | source)
XLA Modules:
  0.0 59.5 jit_solution(10910194505200474930)
XLA Ops:
  0.6 55.0 %shard_map.77 = (bf16[16,32,64,64]{3,2,1,0:T(8,128)(2,1)S(1)}, bf16[16,32,32,64]{3,2,1,0:T(8,128)(2,1)S(1)}, f32[32,64,64]{2,1,0:T(8,128)S(1)}, f32[32,32,64]{2,1,0:T(8,128)S(1)}) custom-call(bf16[16,2,32,32,64]{4,3,2,1,0:T(8,128)(2,1)} %frames.1, bf16[3,3,64,256]{3,2,1,0:T(8,128)(2,1)} %w_x.1, bf16[3,3,64,256]{3,2,1,0:T(8,128)(2,1)} %w_h.1, ...), custom_call_target="tpu_custom_call" | custom-call | tf_op jit(solution)/shard_map/pallas_call | solution.py:298
  55.6 3.6 %shard_map.78 = (bf16[16,2,32,32,64]{4,3,2,1,0:T(8,128)(2,1)}, f32[2,32,32,64]{3,2,1,0:T(8,128)}) custom-call(bf16[16,32,64,64]{3,2,1,0:T(8,128)(2,1)S(1)} %get-tuple-element.6.hout, bf16[16,32,32,64]{3,2,1,0:T(8,128)(2,1)S(1)} %get-tuple-element.7.hpeer, f32[32,64,64]{2,1,0:T(8,128)S(1)} %get-tuple-element.8.cout, f32[32,32,64]{2,1,0:T(8,128)S(1)} %get-tuple-element.9.cpeer), custom_call_target="tpu_custom_call" | custom-call | tf_op jit(solution)/shard_map/pallas_call | solution.py:314

commit v3 on v2

--- a/solution.py
+++ b/solution.py
@@ -13,6 +13,7 @@
 PIECE = 4
 RING = 8
 BLOCKS = (4, 4, 4, 4)
+FILL = (1, 1, 1, 1)
 
 
 def cuts(lo, hi, size=PIECE):
@@ -37,9 +38,9 @@
 
 
 def kernel(plan, n_rows, frames, w_x, w_h, bias, h_init, c_init, hout, hpeer, cout, cpeer,
-           xin, hst, cst, xh_even, xh_odd, cbuf, shift, wbuf,
+           hgo, cgo, xgo, xin, hst, cst, xh_even, xh_odd, cbuf, shift, wbuf,
            xs_ref, xr_ref, hs_ref, hr_ref, cs_ref, cr_ref,
-           s_w, s_i, s_ir, s_is, s_x, s_xr, s_xs, s_b, s_bs, s_or, s_os, s_c):
+           s_w, s_i, s_ir, s_is, s_x, s_xr, s_xs, s_b, s_bs, s_or, s_os):
     T, R, W, HW = plan.T, plan.R, plan.W, plan.HW
     PAD = plan.K
     NB = len(plan.blocks)
@@ -59,26 +60,43 @@
             src_ref=src, dst_ref=dst, send_sem=ssem, recv_sem=rsem, device_id=dev, device_id_type=MESH)
 
     peer = {"cols": p}
-    side_dev = [{"rows": lax.rem(n + n_rows - 1, n_rows)}, {"rows": lax.rem(n + 1, n_rows)}]
-
-    w_copies = [local(w_h, wbuf.at[:, :, 0], s_w.at[0]), local(w_x, wbuf.at[:, :, 1], s_w.at[1])]
+    side_dev = [{"rows": n - 1}, {"rows": n + 1}]
+    side_ok = [has_up, has_dn]
+
+    def each_side(do):
+        for side in range(2):
+            @pl.when(side_ok[side])
+            def _():
+                do(side)
+
+    barrier = pltpu.get_barrier_semaphore()
+
+    def signal(dev):
+        pl.semaphore_signal(barrier, inc=1, device_id=dev, device_id_type=MESH)
+
+    signal(peer)
+    each_side(lambda side: signal(side_dev[side]))
+
     h_own = local(h_init.at[s], hst.at[:, mine], s_i.at[0])
     c_own = local(c_init.at[s], cst.at[:, mine], s_i.at[1])
     x_own = [local(frames.at[a:e, s], xin.at[a:e, :, mine], s_x.at[g]) for g, (a, e) in enumerate(plan.groups)]
-    for c in [h_own, c_own, x_own[0], *w_copies, *x_own[1:]]:
+    h_got = local(h_init.at[p], hgo, s_i.at[2])
+    c_got = local(c_init.at[p], cgo, s_i.at[3])
+    x_got = [local(frames.at[a:e, p], xgo.at[a:e], s_i.at[4 + g]) for g, (a, e) in enumerate(plan.groups[:2])]
+    w_copies = [local(w_h, wbuf.at[:, :, 0], s_w.at[0]), local(w_x, wbuf.at[:, :, 1], s_w.at[1])]
+    for c in [h_got, x_got[0], h_own, x_own[0], c_got, c_own, x_got[1], x_own[1], *w_copies, *x_own[2:]]:
         c.start()
-
-    barrier = pltpu.get_barrier_semaphore()
-    for dev in [peer, *side_dev]:
-        pl.semaphore_signal(barrier, inc=1, device_id=dev, device_id_type=MESH)
-    pl.semaphore_wait(barrier, 3)
-
-    h_push = remote(h_init.at[p], hst.at[:, mine], s_is.at[0], s_ir.at[0], peer)
-    c_push = remote(c_init.at[p], cst.at[:, mine], s_is.at[1], s_ir.at[1], peer)
-    x_push = [remote(frames.at[a:e, p], xin.at[a:e, :, mine], s_xs.at[g], s_xr.at[g], peer)
+    pl.semaphore_wait(barrier, 1 + has_up.astype(jnp.int32) + has_dn.astype(jnp.int32))
+
+    h_push = remote(hgo, hst.at[:, mine], s_is.at[0], s_ir.at[0], peer)
+    c_push = remote(cgo, cst.at[:, mine], s_is.at[1], s_ir.at[1], peer)
+    x_push = [remote((xgo if g < 2 else frames.at[:, p]).at[a:e], xin.at[a:e, :, mine], s_xs.at[g], s_xr.at[g], peer)
               for g, (a, e) in enumerate(plan.groups)]
-    for c in [h_push, c_push, *x_push]:
-        c.start()
+    for got, push in [(h_got, h_push), (x_got[0], x_push[0]), (c_got, c_push), (x_got[1], x_push[1])]:
+        got.wait()
+        push.start()
+    for push in x_push[2:]:
+        push.start()
 
     shift[...] = jnp.zeros_like(shift)
     low = lax.broadcasted_iota(jnp.int32, (1, LANES), 1) < CH
@@ -152,7 +170,7 @@
                 m = plan.xrows[t]
                 lo = 0 if side == 0 else R - m
                 xs_ref[side, plan.xat[t]:plan.xat[t] + m] = pack(xin[t, lo:lo + m])
-            border(b, 0, side).start()
+        each_side(lambda side: border(b, 0, side).start())
 
     def send_state(b, h_rows):
         k = plan.blocks[b]
@@ -162,9 +180,11 @@
             lo = PAD if side == 0 else PAD + R - (k - 1)
             c = cbuf[lo:lo + k - 1]
             cs_ref[side, plan.cat[b]:plan.cat[b] + k - 1] = jnp.where(low_half, c[:, :HW], c[:, HW:])
-        for side in range(2):
+        def start(side):
             border(b, 1, side).start()
             border(b, 2, side).start()
+
+        each_side(start)
 
     weights = wbuf[...].reshape(9 * LANES, 4 * CH)
 
@@ -206,40 +226,53 @@
         while pending:
             cells(*pending.pop())
 
-    def out_peer(t0, t1, g):
-        return remote(hout.at[t0:t1, :, theirs], hpeer.at[t0:t1], s_os.at[g], s_or.at[g], peer)
-
-    h_own.wait()
-    h_push.wait_recv()
-    c_own.wait()
-    c_push.wait_recv()
+    outs = []
+
+    def push_h(t0, t1, lo=0, hi=R):
+        g = len(outs)
+        rows = slice(lo, hi)
+        outs.append(remote(hout.at[t0:t1, rows, theirs], hpeer.at[t0:t1, rows], s_os.at[g], s_or.at[g], peer))
+        outs[-1].start()
+
+    def push_c(lo, hi):
+        g = len(outs)
+        outs.append(remote(cout.at[lo:hi, theirs], cpeer.at[lo:hi], s_os.at[g], s_or.at[g], peer))
+        outs[-1].start()
+
+    for c in [h_own, c_own]:
+        c.wait()
+    for c in [h_push, c_push]:
+        c.wait_recv()
     c0 = cst[...]
     cbuf[PAD:PAD + R] = jnp.concatenate([c0, c0], axis=2)
     send_state(0, hst)
     wait_x(0)
-    wait_x(1)
-    send_x(0)
     for lo, hi in cuts(0, R):
         emit(0, lo, hi, jnp.concatenate([hst[lo:hi].astype(f32), x_rows(0, lo, hi)], axis=2))
 
-    outs = []
     for b, k in enumerate(plan.blocks):
         f = plan.first[b]
-        for o in range(k):
-            t = f + o
+        last = b + 1 == NB
+
+        def inner(o):
             if o == 0:
-                inner = [(1, k + 1), *cuts(k + 1, R - 1 - k), (R - 1 - k, R - 1)]
+                got = [(1, k + 1), *cuts(k + 1, R - 1 - k), (R - 1 - k, R - 1)]
             else:
-                inner = cuts(o + 1, R - 1 - o)
-            for i, (lo, hi) in enumerate(inner[1:-1] + [inner[0], inner[-1]]):
-                piece(t, lo, hi)
-                if b and o == 0 and i == 0:
-                    send_state(b, hout.at[f - 1])
-                    outs.append(out_peer(plan.first[b - 1], f, b - 1))
-                    outs[-1].start()
-        for kind in (1, 2, 0):
-            for side in range(2):
-                border(b, kind, side).wait_recv()
+                got = cuts(o + 1, R - 1 - o)
+            return [(f + o, lo, hi) for lo, hi in got[1:-1] + [got[0], got[-1]]]
+
+        fill = FILL[b]
+        for o in range(k - fill):
+            for i, at in enumerate(inner(o)):
+                piece(*at)
+                if o == 0 and i == 0:
+                    if b == 0:
+                        wait_x(1)
+                        send_x(0)
+                    else:
+                        send_state(b, hout.at[f - 1])
+                        push_h(plan.first[b - 1], f)
+        each_side(lambda side: [border(b, kind, 1 - side).wait_recv() for kind in (1, 2, 0)])
         wait_x(b + 2)
         for side in range(2):
             lo = -k if side == 0 else R
@@ -249,26 +282,33 @@
             packed = cr_ref[side, plan.cat[b]:plan.cat[b] + k - 1]
             cbuf[lo:lo + k - 1, 0:HW] = packed
             cbuf[lo:lo + k - 1, HW:W] = pltpu.roll(packed, CH, 2)
-        if b + 1 < NB:
+        if not last:
             send_x(b + 1)
+        rest = inner(k - 1) if fill else []
         for o in range(k):
             m = k - 1 - o
-            for (a, e), (a2, e2) in zip(cuts(-m, o + 1, max(PIECE, k)), cuts(R - 1 - o, R + m, max(PIECE, k))):
+            edges = zip(cuts(-m, o + 1, max(PIECE, k)), cuts(R - 1 - o, R + m, max(PIECE, k)))
+            for (a, e), (a2, e2) in edges:
                 piece(f + o, a, e)
                 piece(f + o, a2, e2)
+            if o < k - 1:
+                part = rest[len(rest) * o // (k - 1):len(rest) * (o + 1) // (k - 1)]
+                for at in part:
+                    piece(*at)
+        if last:
+            push_h(f, T - 1)
+            push_h(T - 1, T, k, R - k)
+            push_c(k, R - k)
     flush()
-    outs.append(out_peer(plan.first[-1], T, NB - 1))
-    outs[-1].start()
-    c_out = remote(cout.at[:, theirs], cpeer, s_c.at[0], s_c.at[1], peer)
-    c_out.start()
+    k = plan.blocks[-1]
+    for lo, hi in ((0, k), (R - k, R)):
+        push_h(T - 1, T, lo, hi)
+        push_c(lo, hi)
 
     for c in [h_push, c_push, *x_push]:
         c.wait_send()
-    for b in range(NB):
-        for kind in range(3):
-            for side in range(2):
-                border(b, kind, side).wait_send()
-    for c in [*outs, c_out]:
+    each_side(lambda side: [border(b, kind, side).wait_send() for b in range(NB) for kind in range(3)])
+    for c in outs:
         c.wait()
 
 
@@ -301,14 +341,15 @@
         in_specs=[hbm, hbm, hbm, vmem, hbm, hbm],
         out_specs=(vmem,) * 4,
         scratch_shapes=[
+            vm((R, HW, CH), bf), vm((R, HW, CH), f32), vm((plan.groups[1][1], R, HW, CH), bf),
             vm((T, R, W, CH), bf), vm((R, W, CH), bf), vm((R, W, CH), f32),
             vm((3, R + 2 * PAD, W, LANES), bf), vm((3, R + 2 * PAD, W, LANES), bf),
             vm((R + 2 * PAD, W, LANES), f32), vm((RING, W + 16, LANES), f32), vm((3, 3, 2, CH, 4 * CH), bf),
             vm((2, plan.xat[-1], HW, LANES), bf), vm((2, plan.xat[-1], HW, LANES), bf),
             vm((2, plan.hat[-1], HW, LANES), bf), vm((2, plan.hat[-1], HW, LANES), bf),
             vm((2, plan.cat[-1], HW, LANES), f32), vm((2, plan.cat[-1], HW, LANES), f32),
-            dma((2,)), dma((2,)), dma((2,)), dma((2,)), dma((G,)), dma((G,)), dma((G,)),
-            dma((3, 2, NB)), dma((3, 2, NB)), dma((NB,)), dma((NB,)), dma((2,))],
+            dma((2,)), dma((6,)), dma((2,)), dma((2,)), dma((G,)), dma((G,)), dma((G,)),
+            dma((3, 2, NB)), dma((3, 2, NB)), dma((NB + 6,)), dma((NB + 6,))],
         compiler_params=pltpu.CompilerParams(collective_id=0, has_side_effects=True, vmem_limit_bytes=46 * 2**20),
     )(frames, w_x, w_h, gate_bias.reshape(1, -1), h_init, c_init)
     return pl.pallas_call(

time: 59.6 us -> 55.1 us (0.924)
  the two profiles are of different devices: /device:TPU:1 before, /device:TPU:97 now
where the time goes in v3:
time: 55.1 us; the launch traced here: 54.9 us
  Pallas kernels  54.1 us (98%)
  between operations  0.82 us (1%)
    pallas_call x1, Pallas kernels, run(): pl.pallas_call(functools.partial(kernel, plan, n_rows), out_shape=(vm((T,...  50.5 us
    pallas_call x1, Pallas kernels, run(): pl.pallas_call(store, out_shape=(jax.ShapeDtypeStruct(frames.shape, bf),...  3.64 us

profile of v3, /device:TPU:97, one launch (start us, length us, event | category | flops | bytes accessed | tf_op | source)
XLA Modules:
  0.0 54.9 jit_solution(8068326395761065878)
XLA Ops:
  0.6 50.5 %shard_map.77 = (bf16[16,32,64,64]{3,2,1,0:T(8,128)(2,1)S(1)}, bf16[16,32,32,64]{3,2,1,0:T(8,128)(2,1)S(1)}, f32[32,64,64]{2,1,0:T(8,128)S(1)}, f32[32,32,64]{2,1,0:T(8,128)S(1)}) custom-call(bf16[16,2,32,32,64]{4,3,2,1,0:T(8,128)(2,1)} %frames.1, bf16[3,3,64,256]{3,2,1,0:T(8,128)(2,1)} %w_x.1, bf16[3,3,64,256]{3,2,1,0:T(8,128)(2,1)} %w_h.1, ...), custom_call_target="tpu_custom_call" | custom-call | tf_op jit(solution)/shard_map/pallas_call | solution.py:338
  51.1 3.6 %shard_map.78 = (bf16[16,2,32,32,64]{4,3,2,1,0:T(8,128)(2,1)}, f32[2,32,32,64]{3,2,1,0:T(8,128)}) custom-call(bf16[16,32,64,64]{3,2,1,0:T(8,128)(2,1)S(1)} %get-tuple-element.6.hout, bf16[16,32,32,64]{3,2,1,0:T(8,128)(2,1)S(1)} %get-tuple-element.7.hpeer, f32[32,64,64]{2,1,0:T(8,128)S(1)} %get-tuple-element.8.cout, f32[32,32,64]{2,1,0:T(8,128)S(1)} %get-tuple-element.9.cpeer), custom_call_target="tpu_custom_call" | custom-call | tf_op jit(solution)/shard_map/pallas_call | solution.py:355
